TPU v7x, 32 devices: a whole 2x2x4 slice. The times are simulated.
32 devices in a mesh: lat: 4 (over z), lon: 8 (over y, x, core).
Axes of the slice: x: 2, y: 2, z: 4, core: 2. Of those that a mesh axis runs over, the one named last changes fastest.
Arguments:
- zonal_wind: float32 [32, 32, 2048], P(None, 'lat', 'lon'), may hold values from -6 to 6
- merid_wind: float32 [32, 32, 2048], P(None, 'lat', 'lon'), may hold values from -6 to 6
- vertical_wind: float32 [32, 32, 2048], P(None, 'lat', 'lon'), may hold values from -6 to 6
- pressure: float32 [32, 32, 2048], P(None, 'lat', 'lon'), may hold values from -6 to 6
- zonal_coef: float32 [32], P('lat'), may hold values from 0.05 to 0.4
- merid_coef: float32 [32], P('lat'), may hold values from 0.05 to 0.4
- level_coef: float32 [32], replicated, may hold values from 0.3 to 1.5
- sound_coef: float32 [32, 32, 2048], P(None, 'lat', 'lon'), may hold values from 0.2 to 2
- cutoff: int32 [32], replicated, may hold values from 1 to 511
- filter_mask: int32 [32], replicated, may hold values from 0 to 1, as said below
Outputs:
- zonal_next: float32 [32, 32, 2048], P(None, 'lat', 'lon')
- merid_next: float32 [32, 32, 2048], P(None, 'lat', 'lon')
- vertical_next: float32 [32, 32, 2048], P(None, 'lat', 'lon')
- pressure_next: float32 [32, 32, 2048], P(None, 'lat', 'lon')
Inputs may be any that keep to these rules, and one draw needn't show every extreme that they name: `filter_mask`: for every latitude j below 16 exactly one of j and j + 16 is filtered; the filtered ones are the first n and the last 16 - n latitudes, for some n from 4 to 12.
All inputs are finite; a program needn't handle non-finite values.
Results may differ from a plain program's by a relative error of at most 0.0001.
Values sent between devices are 32-bit elements; how exact they have to be, the bound alone decides.
No kernel may reach another device: no remote copies, remote signals or barrier semaphores. Data moves between devices by JAX's collectives and lax.ppermute only.
A program may use at most 64 MiB of HBM per device.

v0:
```python
import math
import jax
import jax.numpy as jnp
from jax import lax
from jax.sharding import PartitionSpec as P

SUBSTEPS = 2


def extended(block, sides, width):
    for axis, dim in sides:
        count = lax.axis_size(axis)
        forward = [(i, i + 1) for i in range(count - 1)]
        forward.append((count - 1, 0))
        backward = [(target, source) for source, target in forward]
        low = lax.ppermute(
            lax.slice_in_dim(block, block.shape[dim] - width, None, axis=dim), axis, forward
        )
        high = lax.ppermute(lax.slice_in_dim(block, 0, width, axis=dim), axis, backward)
        block = jnp.concatenate([low, block, high], axis=dim)
    return block


def rim_fix(padded, lat_dim):
    band_index = lax.axis_index("lat")
    bands = lax.axis_size("lat")
    extent = padded.shape[lat_dim]
    position = lax.broadcasted_iota(jnp.int32, padded.shape, lat_dim)
    first_edge = jnp.logical_and(position == 0, band_index == 0)
    final_edge = jnp.logical_and(position == extent - 1, band_index == bands - 1)
    return jnp.where(jnp.logical_or(first_edge, final_edge), 0.0, padded)


def dft_tables(length):
    half_len = length // 2
    sample = lax.broadcasted_iota(jnp.int32, (length, length), 0)
    column = lax.broadcasted_iota(jnp.int32, (length, length), 1)
    is_cosine = column <= half_len
    wavenum = jnp.where(is_cosine, column, column - half_len)
    phase = sample * wavenum % length
    angle = 2.0 * math.pi / length * phase.astype(jnp.float32)
    forward = jnp.where(is_cosine, jnp.cos(angle), jnp.sin(angle))
    single = jnp.logical_and(is_cosine, jnp.logical_or(wavenum == 0, wavenum == half_len))
    weight = jnp.where(single, 1.0, 2.0) / length
    inverse = jnp.transpose(forward * weight)
    wave_row = wavenum[0].astype(jnp.float32)
    return (forward, inverse, wave_row)


def damping(wave_row, limits):
    bound_col = limits[:, None]
    ratio = bound_col / jnp.maximum(wave_row[None, :], 1.0)
    return jnp.where(wave_row[None, :] > bound_col, ratio * ratio, 1.0)


def transform_band(block, limits, forward, inverse, wave_row):
    circles = lax.all_to_all(block, "lon", split_axis=1, concat_axis=3, tiled=True)
    spectra = jnp.einsum("vetj,jc->vetc", circles, forward, precision=lax.Precision.HIGHEST)
    scaled = spectra * damping(wave_row, limits)
    damped = jnp.einsum("vetc,cj->vetj", scaled, inverse, precision=lax.Precision.HIGHEST)
    return lax.all_to_all(damped, "lon", split_axis=3, concat_axis=1, tiled=True)


def filtered_increments(increments, own_flags, own_limits, forward, inverse, wave_row):
    flag_cols = own_flags[:, None]
    damped = transform_band(increments, own_limits, forward, inverse, wave_row)
    return jnp.where(flag_cols, damped, increments)


def column_solve(vertical_wind, pstar, level_coef, sound_coef):
    levels = vertical_wind.shape[0]
    zero_slab = jnp.zeros_like(vertical_wind[0])
    ratios = []
    values = []
    prev_ratio = zero_slab
    prev_value = zero_slab
    for level in range(levels):
        alpha = level_coef[level]
        below = alpha * sound_coef[level]
        if level + 1 < levels:
            above = alpha * sound_coef[level + 1]
            rhs = vertical_wind[level] - alpha * (pstar[level + 1] - pstar[level])
        else:
            above = zero_slab
            rhs = vertical_wind[level] + alpha * pstar[level]
        pivot = 1.0 + below + above + below * prev_ratio
        prev_ratio = -above / pivot
        prev_value = (rhs + below * prev_value) / pivot
        ratios.append(prev_ratio)
        values.append(prev_value)
    solved = [zero_slab] * levels
    upper_value = values[levels - 1]
    solved[levels - 1] = upper_value
    for level in range(levels - 2, -1, -1):
        upper_value = values[level] - ratios[level] * upper_value
        solved[level] = upper_value
    new_wind = jnp.stack(solved)
    wind_below = jnp.concatenate([zero_slab[None], new_wind[:-1]], axis=0)
    new_pressure = pstar - sound_coef * (new_wind - wind_below)
    return (new_wind, new_pressure)


def body(
    zonal_wind,
    merid_wind,
    vertical_wind,
    pressure,
    zonal_coef,
    merid_coef,
    level_coef,
    sound_coef,
    cutoff,
    filter_mask,
):
    lat_rows = pressure.shape[1]
    start = lax.axis_index("lat") * lat_rows
    own_flags = lax.dynamic_slice_in_dim(filter_mask, start, lat_rows) > 0
    own_limits = lax.dynamic_slice_in_dim(cutoff, start, lat_rows).astype(jnp.float32)
    forward, inverse, wave_row = dft_tables(pressure.shape[2] * lax.axis_size("lon"))
    zonal_rows = zonal_coef[None, :, None]
    merid_rows = merid_coef[None, :, None]
    for step in range(SUBSTEPS):
        padded = extended(pressure, (("lat", 1), ("lon", 2)), 1)
        padded = rim_fix(padded, 1)
        zonal_step = -zonal_rows * (padded[:, 1:-1, 2:] - padded[:, 1:-1, :-2])
        merid_step = -merid_rows * (padded[:, 2:, 1:-1] - padded[:, :-2, 1:-1])
        increments = jnp.stack([zonal_step, merid_step])
        damped = filtered_increments(increments, own_flags, own_limits, forward, inverse, wave_row)
        winds = jnp.stack([zonal_wind, merid_wind]) + damped
        wind_pad = extended(winds, (("lat", 2), ("lon", 3)), 1)
        wind_pad = rim_fix(wind_pad, 2)
        diverge = zonal_rows * (wind_pad[0, :, 1:-1, 2:] - wind_pad[0, :, 1:-1, :-2])
        diverge = diverge + merid_rows * (wind_pad[1, :, 2:, 1:-1] - wind_pad[1, :, :-2, 1:-1])
        pstar = pressure - sound_coef * diverge
        vertical_wind, pressure = column_solve(vertical_wind, pstar, level_coef, sound_coef)
        zonal_wind = winds[0]
        merid_wind = winds[1]
    return (zonal_wind, merid_wind, vertical_wind, pressure)


def solution(mesh):
    in_specs = (
        P(None, "lat", "lon"),
        P(None, "lat", "lon"),
        P(None, "lat", "lon"),
        P(None, "lat", "lon"),
        P("lat"),
        P("lat"),
        P(),
        P(None, "lat", "lon"),
        P(),
        P(),
    )
    out_specs = (
        P(None, "lat", "lon"),
        P(None, "lat", "lon"),
        P(None, "lat", "lon"),
        P(None, "lat", "lon"),
    )
    return jax.shard_map(body, mesh=mesh, in_specs=in_specs, out_specs=out_specs, check_vma=False)
```

profile of v0, /device:TPU:0, one launch (start us, length us, event | category | flops | bytes accessed | tf_op | source)
XLA Modules:
  0.0 585.0 jit_solution(11969171518378575389)
XLA Ops:
  1.8 5.1 collective-permute-start.1
  9.1 3.5 collective-permute-done
  13.5 6.0 %collective-permute-done.3 = f32[32,10,1]{2,1,0:T(8,128)S(1)} collective-permute-done((f32[32,10,1]{2,1,0:T(8,128)S(1)}, f32[32,10,1]{2,1,0:T(8,128)S(1)}, u32[]{:S(2)}, u32[]{:S(2)}) %collective-permute-start.3) | collective-permute-done | bytes 1312 | tf_op jit(solution)/shard_map/ppermute | solution.py:19
  19.5 3.0 collective-permute-done.2
  24.2 3.8 all-to-all-start
  28.2 9.5 %all-to-all-done = f32[2,32,8,256]{3,2,0,1:T(8,128)S(1)} async-done(((f32[2,32,8,256]{3,2,0,1:T(8,128)}), f32[2,32,8,256]{3,2,0,1:T(8,128)S(1)}, u32[]{:S(2)}, u32[]{:S(2)}) %all-to-all-start) | async-done | bytes 524320 | tf_op jit(solution)/shard_map/all_to_all | solution.py:57
  38.0 75.8 %fusion.15 = f32[2,4,8,2048]{3,2,1,0:T(8,128)S(1)} fusion(f32[2,4,8,2048]{3,2,1,0:T(8,128)S(1)} %all_to_all.55, s32[2048]{0:T(1024)S(1)} %iota_add_fusion, pred[2048]{0:T(1024)(128)(4,1)S(1)} %iota_compare_fusion, f32[8,2048]{1,0:T(8,128)S(1)} %fusion.44), kind=kOutput, calls=%fused_computation.21 | convolution fusion | flops 3288465408 | bytes 1124352 | tf_op jit(solution)/shard_map/vetj,jc->vetc/dot_general | solution.py:58
  113.9 82.4 %fusion.5 = f32[2,4,8,2048]{3,2,1,0:T(8,128)S(1)} fusion(f32[2,4,8,2048]{3,2,1,0:T(8,128)S(1)} %fusion.15, s32[2048]{0:T(1024)S(1)} %iota_add_fusion, pred[2048]{0:T(1024)(128)(4,1)S(1)} %iota_compare_fusion), kind=kOutput, calls=%fused_computation.8 | convolution fusion | flops 3317694464 | bytes 1058816 | tf_op jit(solution)/shard_map/vetc,cj->vetj/dot_general | solution.py:60
  196.4 5.8 copy.23
  202.1 12.3 %reshape.77 = f32[8,1,16384]{2,1,0:T(1,128)} reshape(f32[2048,2,4,8]{3,2,1,0:T(4,128)} %bitcast.161) | data formatting | bytes 1048576
  214.4 3.6 all-to-all-start.1
  218.1 9.6 %all-to-all-done.1 = f32[8,1,16384]{2,1,0:T(1,128)S(1)} async-done(((f32[8,1,16384]{2,1,0:T(1,128)}), f32[8,1,16384]{2,1,0:T(1,128)S(1)}, u32[]{:S(2)}, u32[]{:S(2)}) %all-to-all-start.1) | async-done | bytes 524320 | tf_op jit(solution)/shard_map/all_to_all | solution.py:61
  230.1 13.2 %reshape.78 = f32[2048,2,4,8]{3,2,1,0:T(4,128)} reshape(f32[8,16384]{1,0:T(8,128)S(1)} %reduce) | data formatting | bytes 1048576
  243.3 6.7 %copy.24 = f32[2,4,8,8,256]{4,2,0,1,3:T(8,128)S(1)} copy(f32[2,4,8,8,256]{2,1,0,4,3:T(4,128)} %bitcast.162) | data formatting | bytes 1048576 | tf_op jit(solution)/shard_map/all_to_all | solution.py:61
  254.5 2.1 collective-permute-done.4
  258.8 10.3 %collective-permute-done.7 = f32[2,32,10,1]{3,2,1,0:T(8,128)S(1)} collective-permute-done((f32[2,32,10,1]{3,2,1,0:T(8,128)S(1)}, f32[2,32,10,1]{3,2,1,0:T(8,128)S(1)}, u32[]{:S(2)}, u32[]{:S(2)}) %collective-permute-start.7) | collective-permute-done | bytes 2592 | tf_op jit(solution)/shard_map/ppermute | solution.py:19
  272.0 20.4 %add_divide_fusion.32 = (f32[1,8,256]{2,1,0:T(8,128)S(1)}, f32[1,8,256]{2,1,0:T(8,128)S(1)}, f32[1,8,256]{2,1,0:T(8,128)S(1)}, f32[1,8,256]{2,1,0:T(8,128)S(1)},...) fusion(f32[32,8,256]{2,1,0:T(8,128)S(1)} %copy-done.6, ...), kind=kLoop, calls=%fused_computation.313 | loop fusion | flops 882688 | bytes 1523836 | tf_op jit(solution)/shard_map/div | solution.py:88
  297.2 2.2 collective-permute-done.9
  302.0 5.6 collective-permute-done.11
  307.6 2.2 collective-permute-done.10
  311.4 12.3 %all_to_all.72 = f32[2,32,8,256]{3,2,0,1:T(8,128)S(1)} all-to-all(f32[2,32,8,256]{3,2,0,1:T(8,128)S(1)} %copy.29), channel_id=1, replica_groups=mesh['lat'=4,'lon'=8] {'lon'}, dimensions={1} | all-to-all | bytes 1048576 | tf_op jit(solution)/shard_map/all_to_all | solution.py:57
  325.0 77.2 %fusion.18 = f32[2,4,8,2048]{3,2,1,0:T(8,128)S(1)} fusion(f32[2,4,8,2048]{3,2,1,0:T(8,128)} %all_to_all.63, s32[2048]{0:T(1024)} %copy-done.21, pred[2048]{0:T(1024)(128)(4,1)} %copy-done.24, f32[8,2048]{1,0:T(8,128)} %copy-done.20), kind=kOutput, calls=%fused_computation.22 | convolution fusion | flops 3288465408 | bytes 1124352 | tf_op jit(solution)/shard_map/vetj,jc->vetc/dot_general | solution.py:58
  402.2 82.1 %fusion.3 = f32[2,4,8,2048]{3,2,1,0:T(8,128)S(1)} fusion(f32[2,4,8,2048]{3,2,1,0:T(8,128)S(1)} %fusion.18, s32[2048]{0:T(1024)S(1)} %copy-done.22, pred[2048]{0:T(1024)(128)(4,1)S(1)} %copy-done.25), kind=kOutput, calls=%fused_computation.6 | convolution fusion | flops 3317694464 | bytes 1058816 | tf_op jit(solution)/shard_map/vetc,cj->vetj/dot_general | solution.py:60
  484.3 5.8 copy.31
  490.1 11.6 %reshape.79 = f32[8,1,16384]{2,1,0:T(1,128)S(1)} reshape(f32[2048,2,4,8]{3,2,1,0:T(4,128)} %bitcast.163) | data formatting | bytes 1048576
  501.7 12.8 %all_to_all.73 = f32[8,1,16384]{2,1,0:T(1,128)} all-to-all(f32[8,1,16384]{2,1,0:T(1,128)S(1)} %reshape.79), channel_id=1, replica_groups=mesh['lat'=4,'lon'=8] {'lon'}, dimensions={0} | all-to-all | bytes 1048576 | tf_op jit(solution)/shard_map/all_to_all | solution.py:61
  514.5 2.9 reduce.1
  517.4 13.2 %reshape.80 = f32[2048,2,4,8]{3,2,1,0:T(4,128)} reshape(f32[8,16384]{1,0:T(8,128)S(1)} %reduce.1) | data formatting | bytes 1048576
  530.7 6.7 %copy.32 = f32[2,4,8,8,256]{4,2,1,3,0:T(8,128)S(1)} copy(f32[2,4,8,8,256]{2,1,0,4,3:T(4,128)} %bitcast.164) | data formatting | bytes 1048576 | tf_op jit(solution)/shard_map/all_to_all | solution.py:61
  540.5 2.9 collective-permute-done.13
  546.8 10.5 %collective-permute-done.15 = f32[2,32,10,1]{3,2,0,1:T(8,128)S(1)} collective-permute-done((f32[2,32,10,1]{3,2,0,1:T(8,128)S(1)}, f32[2,32,10,1]{3,2,0,1:T(8,128)S(1)}, u32[]{:S(2)}, u32[]{:S(2)}) %collective-permute-start.15) | collective-permute-done | bytes 2592 | tf_op jit(solution)/shard_map/ppermute | solution.py:19
  561.3 20.7 %add_divide_fusion.1 = (f32[1,8,256]{2,1,0:T(8,128)S(1)}, f32[1,8,256]{2,1,0:T(8,128)S(1)}, f32[1,8,256]{2,1,0:T(8,128)S(1)}, f32[1,8,256]{2,1,0:T(8,128)S(1)}, ...) fusion(f32[1,8,256]{2,1,0:T(8,128)S(1)} %get-tuple-element.102,, ...), kind=kLoop, calls=%fused_computation.248 | loop fusion | flops 452608 | bytes 1269884 | tf_op jit(solution)/shard_map/div | solution.py:88
  (199 shorter events, 41.2 us)
Async XLA Ops:
  1.8 7.3 %collective-permute-start.1 = (f32[32,1,256]{2,1,0:T(1,128)S(1)}, f32[32,1,256]{2,1,0:T(1,128)S(1)}, u32[]{:S(2)}, u32[]{:S(2)}) collective-permute-start(f32[32,1,256]{2,1,0:T(1,128)S(1)} %get-tuple-element.213), channel_id=1, source_target_pairs={{8,0},{16,8},{24,16},{0,24},{9,1},{17,9},{25,17},{1,25},{10,2},{18... | collective-permute-start | bytes 98312 | tf_op jit(solution)/shard_map/ppermute | solution.py:19
  6.9 5.7 collective-permute-start
  6.9 106.9 %copy-start.21 = (s32[2048]{0:T(1024)}, s32[2048]{0:T(1024)S(1)}, u32[]{:S(2)}) copy-start(s32[2048]{0:T(1024)S(1)} %iota_add_fusion) | copy-start | bytes 24580
  6.9 106.9 %copy-start.24 = (pred[2048]{0:T(1024)(128)(4,1)}, pred[2048]{0:T(1024)(128)(4,1)S(1)}, u32[]{:S(2)}) copy-start(pred[2048]{0:T(1024)(128)(4,1)S(1)} %iota_compare_fusion) | copy-start | bytes 6148
  12.9 6.7 %collective-permute-start.3 = (f32[32,10,1]{2,1,0:T(8,128)S(1)}, f32[32,10,1]{2,1,0:T(8,128)S(1)}, u32[]{:S(2)}, u32[]{:S(2)}) collective-permute-start(f32[32,10,1]{2,1,0:T(8,128)S(1)} %get-tuple-element.209), channel_id=1, source_target_pairs={{1,0},{2,1},{3,2},{4,3},{5,4},{6,5},{7,6},{0,7},{9,8},{10,9},{11,1... | collective-permute-start | bytes 3848 | tf_op jit(solution)/shard_map/ppermute | solution.py:19
  13.4 9.2 %collective-permute-start.2 = (f32[32,10,1]{2,1,0:T(8,128)S(1)}, f32[32,10,1]{2,1,0:T(8,128)S(1)}, u32[]{:S(2)}, u32[]{:S(2)}) collective-permute-start(f32[32,10,1]{2,1,0:T(8,128)S(1)} %get-tuple-element.208), channel_id=1, source_target_pairs={{0,1},{1,2},{2,3},{3,4},{4,5},{5,6},{6,7},{7,0},{8,9},{9,10},{10,1... | collective-permute-start | bytes 3848 | tf_op jit(solution)/shard_map/ppermute | solution.py:16
  13.4 296.4 %copy-start.26 = (pred[10]{0:T(512)(128)(4,1)}, pred[10]{0:T(512)(128)(4,1)S(1)}, u32[]{:S(2)}) copy-start(pred[10]{0:T(512)(128)(4,1)S(1)} %and_or_fusion) | copy-start | bytes 34
  13.5 100.4 %copy-start.29 = (f32[8]{0:T(128)}, f32[8]{0:T(128)S(1)}, u32[]{:S(2)}) copy-start(f32[8]{0:T(128)S(1)} %neg.2118) | copy-start | bytes 100
  13.5 100.4 %copy-start.30 = (f32[8]{0:T(128)}, f32[8]{0:T(128)S(1)}, u32[]{:S(2)}) copy-start(f32[8]{0:T(128)S(1)} %neg.2119) | copy-start | bytes 100
  24.2 13.4 %all-to-all-start = ((f32[2,32,8,256]{3,2,0,1:T(8,128)}), f32[2,32,8,256]{3,2,0,1:T(8,128)S(1)}, u32[]{:S(2)}, u32[]{:S(2)}) async-start(f32[2,32,8,256]{3,2,0,1:T(8,128)} %pad_maximum_fusion.3), calls=%async_computation | async-start | bytes 1048576 | tf_op jit(solution)/shard_map/all_to_all | solution.py:57
  28.2 85.7 %copy-start.20 = (f32[8,2048]{1,0:T(8,128)}, f32[8,2048]{1,0:T(8,128)S(1)}, u32[]{:S(2)}) copy-start(f32[8,2048]{1,0:T(8,128)S(1)} %fusion.44) | copy-start | bytes 196612
  196.3 53.7 %copy-start.1 = (f32[32,8,256]{2,1,0:T(8,128)S(1)}, f32[32,8,256]{2,1,0:T(8,128)}, u32[]{:S(2)}) copy-start(f32[32,8,256]{2,1,0:T(8,128)} %param.11) | copy-start | bytes 786436
  196.3 53.7 %copy-start.2 = (f32[32,8,256]{2,1,0:T(8,128)S(1)}, f32[32,8,256]{2,1,0:T(8,128)}, u32[]{:S(2)}) copy-start(f32[32,8,256]{2,1,0:T(8,128)} %param.10) | copy-start | bytes 786436
  202.1 50.2 %copy-start.4 = (f32[32]{0:T(128)S(1)}, f32[32]{0:T(128)}, u32[]{:S(2)}) copy-start(f32[32]{0:T(128)} %param.16) | copy-start | bytes 388
  214.4 57.3 %copy-start = (f32[32,8,256]{2,1,0:T(8,128)S(1)}, f32[32,8,256]{2,1,0:T(8,128)}, u32[]{:S(2)}) copy-start(f32[32,8,256]{2,1,0:T(8,128)} %param.17) | copy-start | bytes 786436
  214.4 57.6 %copy-start.6 = (f32[32,8,256]{2,1,0:T(8,128)S(1)}, f32[32,8,256]{2,1,0:T(8,128)}, u32[]{:S(2)}) copy-start(f32[32,8,256]{2,1,0:T(8,128)} %param.12) | copy-start | bytes 786436
  214.4 13.3 %all-to-all-start.1 = ((f32[8,1,16384]{2,1,0:T(1,128)}), f32[8,1,16384]{2,1,0:T(1,128)S(1)}, u32[]{:S(2)}, u32[]{:S(2)}) async-start(f32[8,1,16384]{2,1,0:T(1,128)} %reshape.77), calls=%async_computation.1 | async-start | bytes 1048576 | tf_op jit(solution)/shard_map/all_to_all | solution.py:61
  218.1 74.3 %copy-start.23 = (pred[8]{0:T(512)(128)(4,1)}, pred[8]{0:T(512)(128)(4,1)S(1)}, u32[]{:S(2)}) copy-start(pred[8]{0:T(512)(128)(4,1)S(1)} %dynamic-slice_compare_fusion) | copy-start | bytes 28
  250.2 4.3 collective-permute-start.5
  250.6 6.1 %collective-permute-start.4 = (f32[2,32,1,256]{3,2,1,0:T(1,128)S(1)}, f32[2,32,1,256]{3,2,1,0:T(1,128)S(1)}, u32[]{:S(2)}, u32[]{:S(2)}) collective-permute-start(f32[2,32,1,256]{3,2,1,0:T(1,128)S(1)} %get-tuple-element.206), channel_id=1, source_target_pairs={{0,8},{8,16},{16,24},{24,0},{1,9},{9,17},{17,25},{25,1},{2,10},{10... | collective-permute-start | bytes 196616 | tf_op jit(solution)/shard_map/ppermute | solution.py:16
  257.2 11.9 %collective-permute-start.7 = (f32[2,32,10,1]{3,2,1,0:T(8,128)S(1)}, f32[2,32,10,1]{3,2,1,0:T(8,128)S(1)}, u32[]{:S(2)}, u32[]{:S(2)}) collective-permute-start(f32[2,32,10,1]{3,2,1,0:T(8,128)S(1)} %get-tuple-element.195), channel_id=1, source_target_pairs={{1,0},{2,1},{3,2},{4,3},{5,4},{6,5},{7,6},{0,7},{9,8},{10,9},{11,1... | collective-permute-start | bytes 7688 | tf_op jit(solution)/shard_map/ppermute | solution.py:19
  257.2 13.3 %collective-permute-start.6 = (f32[2,32,10,1]{3,2,1,0:T(8,128)S(1)}, f32[2,32,10,1]{3,2,1,0:T(8,128)S(1)}, u32[]{:S(2)}, u32[]{:S(2)}) collective-permute-start(f32[2,32,10,1]{3,2,1,0:T(8,128)S(1)} %get-tuple-element.194), channel_id=1, source_target_pairs={{0,1},{1,2},{2,3},{3,4},{4,5},{5,6},{6,7},{7,0},{8,9},{9,10},{10,1... | collective-permute-start | bytes 7688 | tf_op jit(solution)/shard_map/ppermute | solution.py:16
  295.1 4.3 collective-permute-start.9
  295.5 5.7 collective-permute-start.8
  301.5 6.1 %collective-permute-start.11 = (f32[32,10,1]{2,1,0:T(8,128)S(1)}, f32[32,10,1]{2,1,0:T(8,128)S(1)}, u32[]{:S(2)}, u32[]{:S(2)}) collective-permute-start(f32[32,10,1]{2,1,0:T(8,128)S(1)} %get-tuple-element.205), channel_id=1, source_target_pairs={{1,0},{2,1},{3,2},{4,3},{5,4},{6,5},{7,6},{0,7},{9,8},{10,9},{11,1... | collective-permute-start | bytes 3848 | tf_op jit(solution)/shard_map/ppermute | solution.py:19
  301.5 8.3 %collective-permute-start.10 = (f32[32,10,1]{2,1,0:T(8,128)S(1)}, f32[32,10,1]{2,1,0:T(8,128)S(1)}, u32[]{:S(2)}, u32[]{:S(2)}) collective-permute-start(f32[32,10,1]{2,1,0:T(8,128)S(1)} %get-tuple-element.204), channel_id=1, source_target_pairs={{0,1},{1,2},{2,3},{3,4},{4,5},{5,6},{6,7},{7,0},{8,9},{9,10},{10,1... | collective-permute-start | bytes 3848 | tf_op jit(solution)/shard_map/ppermute | solution.py:16
  325.0 77.2 %copy-start.22 = (s32[2048]{0:T(1024)S(1)}, s32[2048]{0:T(1024)}, u32[]{:S(2)}) copy-start(s32[2048]{0:T(1024)} %copy-done.21) | copy-start | bytes 24580
  325.0 77.2 %copy-start.25 = (pred[2048]{0:T(1024)(128)(4,1)S(1)}, pred[2048]{0:T(1024)(128)(4,1)}, u32[]{:S(2)}) copy-start(pred[2048]{0:T(1024)(128)(4,1)} %copy-done.24) | copy-start | bytes 6148
  538.4 5.0 collective-permute-start.13
  538.7 6.1 %collective-permute-start.12 = (f32[2,32,1,256]{3,2,0,1:T(1,128)S(1)}, f32[2,32,1,256]{3,2,0,1:T(1,128)S(1)}, u32[]{:S(2)}, u32[]{:S(2)}) collective-permute-start(f32[2,32,1,256]{3,2,0,1:T(1,128)S(1)} %get-tuple-element.200), channel_id=1, source_target_pairs={{0,8},{8,16},{16,24},{24,0},{1,9},{9,17},{17,25},{25,1},{2,10},{10... | collective-permute-start | bytes 196616 | tf_op jit(solution)/shard_map/ppermute | solution.py:16
  545.2 12.1 %collective-permute-start.15 = (f32[2,32,10,1]{3,2,0,1:T(8,128)S(1)}, f32[2,32,10,1]{3,2,0,1:T(8,128)S(1)}, u32[]{:S(2)}, u32[]{:S(2)}) collective-permute-start(f32[2,32,10,1]{3,2,0,1:T(8,128)S(1)} %get-tuple-element.193), channel_id=1, source_target_pairs={{1,0},{2,1},{3,2},{4,3},{5,4},{6,5},{7,6},{0,7},{9,8},{10,9},{11,1... | collective-permute-start | bytes 7688 | tf_op jit(solution)/shard_map/ppermute | solution.py:19
  545.3 13.3 %collective-permute-start.14 = (f32[2,32,10,1]{3,2,0,1:T(8,128)S(1)}, f32[2,32,10,1]{3,2,0,1:T(8,128)S(1)}, u32[]{:S(2)}, u32[]{:S(2)}) collective-permute-start(f32[2,32,10,1]{3,2,0,1:T(8,128)S(1)} %get-tuple-element.192), channel_id=1, source_target_pairs={{0,1},{1,2},{2,3},{3,4},{4,5},{5,6},{6,7},{7,0},{8,9},{9,10},{10,1... | collective-permute-start | bytes 7688 | tf_op jit(solution)/shard_map/ppermute | solution.py:16
  (19 other events, 467.6 us)
where the time goes:
time: 589 us; the launch traced here: 585 us
  matrix products  318 us (54%)
  local copies, waits for them, and re-layouts  82 us (14%)
  waiting for transfers between devices  74.9 us (13%)
  other arithmetic  61.9 us (11%)
  blocking collectives  25.1 us (4%)
  starting transfers between devices  21.6 us (4%)
    dot_general x2, matrix products, transform_band(): jnp.einsum('vetc,cj->vetj', scaled, inverse, precision=lax.Precision.HIGH...  165 us
    dot_general x2, matrix products, transform_band(): jnp.einsum('vetj,jc->vetc', circles, forward, precision=lax.Precision.HIG...  153 us
    unnamed x129, local copies, waits for them, and re-layouts  50.8 us
    div x2, other arithmetic, column_solve(): prev_value = (rhs + below * prev_value) / pivot  41.1 us
    ppermute x8, waiting for transfers between devices, extended(): lax.ppermute(lax.slice_in_dim(block, 0, width, axis=dim), axis, backward)  39.1 us
    ppermute x8, waiting for transfers between devices, extended(): lax.ppermute(lax.slice_in_dim(block, block.shape[dim] - width, None, axis...  16.8 us
    all_to_all x3, local copies, waits for them, and re-layouts, transform_band(): lax.all_to_all(damped, 'lon', split_axis=3, concat_axis=1, tiled=True)  13.9 us
    all_to_all x1, blocking collectives, transform_band(): lax.all_to_all(damped, 'lon', split_axis=3, concat_axis=1, tiled=True)  12.8 us
  transfers between devices with their start and end apart: 18, of which 17 were waited for; matrix products, arithmetic and copies ran while one was open for 1% of the time, Pallas kernels for 0%

commit v1 on v0

--- a/solution.py
+++ b/solution.py
@@ -58,7 +58,10 @@
     spectra = jnp.einsum("vetj,jc->vetc", circles, forward, precision=lax.Precision.HIGHEST)
     scaled = spectra * damping(wave_row, limits)
     damped = jnp.einsum("vetc,cj->vetj", scaled, inverse, precision=lax.Precision.HIGHEST)
-    return lax.all_to_all(damped, "lon", split_axis=3, concat_axis=1, tiled=True)
+    return jnp.concatenate(
+        lax.all_to_all(jnp.stack(jnp.split(damped, lax.axis_size("lon"), axis=3)), "lon", 0, 0),
+        axis=1,
+    )
 
 
 def filtered_increments(increments, own_flags, own_limits, forward, inverse, wave_row):

time: 589 us -> 511 us (0.87)
  local copies, waits for them, and re-layouts: 82 us -> 12.5 us
  other arithmetic: 61.9 us -> 53.9 us
    unnamed x129 -> x215, local copies, waits for them, and re-layouts: 50.8 us -> 4.98 us
    all_to_all x3 -> x0, local copies, waits for them, and re-layouts: 13.9 us -> none  [transform_band(): lax.all_to_all(damped, 'lon', split_axis=3, concat_axis=1, tiled=True)]
    dot_general x2 -> x0, local copies, waits for them, and re-layouts: 11.5 us -> none  [transform_band(): jnp.einsum('vetc,cj->vetj', scaled, inverse, precision=lax.Precision.HIGH...]
where the time goes in v1:
time: 511 us; the launch traced here: 507 us
  matrix products  317 us (62%)
  waiting for transfers between devices  75.3 us (15%)
  other arithmetic  53.9 us (11%)
  blocking collectives  24.4 us (5%)
  starting transfers between devices  21.1 us (4%)
  local copies, waits for them, and re-layouts  12.5 us (2%)
    dot_general x2, matrix products, transform_band(): jnp.einsum('vetc,cj->vetj', scaled, inverse, precision=lax.Precision.HIGH...  164 us
    dot_general x2, matrix products, transform_band(): jnp.einsum('vetj,jc->vetc', circles, forward, precision=lax.Precision.HIG...  153 us
    div x2, other arithmetic, column_solve(): prev_value = (rhs + below * prev_value) / pivot  40.4 us
    ppermute x8, waiting for transfers between devices, extended(): lax.ppermute(lax.slice_in_dim(block, 0, width, axis=dim), axis, backward)  39.7 us
    ppermute x8, waiting for transfers between devices, extended(): lax.ppermute(lax.slice_in_dim(block, block.shape[dim] - width, None, axis...  16.5 us
    all_to_all x1, blocking collectives, transform_band(): lax.all_to_all(block, 'lon', split_axis=1, concat_axis=3, tiled=True)  12.3 us
    all_to_all x1, blocking collectives, transform_band(): lax.all_to_all(jnp.stack(jnp.split(damped, lax.axis_size('lon'), axis=3))...  12.1 us
  transfers between devices with their start and end apart: 18, of which 17 were waited for; matrix products, arithmetic and copies ran while one was open for 1% of the time, Pallas kernels for 0%

profile of v1, /device:TPU:0, one launch (start us, length us, event | category | flops | bytes accessed | tf_op | source)
XLA Modules:
  0.0 507.3 jit_solution(1169410655252019513)
XLA Ops:
  1.8 5.1 %collective-permute-start.1 = (f32[32,1,256]{2,1,0:T(1,128)S(1)}, f32[32,1,256]{2,1,0:T(1,128)S(1)}, u32[]{:S(2)}, u32[]{:S(2)}) collective-permute-start(f32[32,1,256]{2,1,0:T(1,128)S(1)} %get-tuple-element.213), channel_id=1, source_target_pairs={{8,0},{16,8},{24,16},{0,24},{9,1},{17,9},{25,17},{1,25},{10,2},{18... | collective-permute-start | bytes 98312 | tf_op jit(solution)/shard_map/ppermute | solution.py:19
  7.0 2.1 iota_select_fusion
  9.1 3.5 collective-permute-done
  13.5 6.1 %collective-permute-done.3 = f32[32,10,1]{2,1,0:T(8,128)S(1)} collective-permute-done((f32[32,10,1]{2,1,0:T(8,128)S(1)}, f32[32,10,1]{2,1,0:T(8,128)S(1)}, u32[]{:S(2)}, u32[]{:S(2)}) %collective-permute-start.3) | collective-permute-done | bytes 1312 | tf_op jit(solution)/shard_map/ppermute | solution.py:19
  19.5 3.0 collective-permute-done.2
  24.3 3.7 all-to-all-start
  28.1 9.5 %all-to-all-done = f32[2,32,8,256]{3,2,0,1:T(8,128)S(1)} async-done(((f32[2,32,8,256]{3,2,0,1:T(8,128)}), f32[2,32,8,256]{3,2,0,1:T(8,128)S(1)}, u32[]{:S(2)}, u32[]{:S(2)}) %all-to-all-start) | async-done | bytes 524320 | tf_op jit(solution)/shard_map/all_to_all | solution.py:57
  38.0 75.8 %fusion.15 = f32[2,4,8,2048]{3,2,1,0:T(8,128)S(1)} fusion(f32[2,4,8,2048]{3,2,1,0:T(8,128)S(1)} %all_to_all.35, s32[2048]{0:T(1024)S(1)} %iota_add_fusion, pred[2048]{0:T(1024)(128)(4,1)S(1)} %iota_compare_fusion, f32[8,2048]{1,0:T(8,128)S(1)} %fusion.43), kind=kOutput, calls=%fused_computation.21 | convolution fusion | flops 3288465408 | bytes 1124352 | tf_op jit(solution)/shard_map/vetj,jc->vetc/dot_general | solution.py:58
  113.9 82.3 %fusion.5 = f32[2,4,8,2048]{3,2,1,0:T(8,128)S(1)} fusion(f32[2,4,8,2048]{3,2,1,0:T(8,128)S(1)} %fusion.15, s32[2048]{0:T(1024)S(1)} %iota_add_fusion, pred[2048]{0:T(1024)(128)(4,1)S(1)} %iota_compare_fusion), kind=kOutput, calls=%fused_computation.8 | convolution fusion | flops 3317694464 | bytes 1058816 | tf_op jit(solution)/shard_map/vetc,cj->vetj/dot_general | solution.py:60
  201.2 3.5 all-to-all-start.1
  204.8 9.6 %all-to-all-done.1 = f32[8,2,4,8,256]{4,3,2,1,0:T(8,128)S(1)} async-done(((f32[8,2,4,8,256]{4,3,2,1,0:T(8,128)}), f32[8,2,4,8,256]{4,3,2,1,0:T(8,128)S(1)}, u32[]{:S(2)}, u32[]{:S(2)}) %all-to-all-start.1) | async-done | bytes 524320 | tf_op jit(solution)/shard_map/all_to_all | solution.py:62
  215.1 1.7 collective-permute-start.4
  217.5 1.5 collective-permute-done.5
  219.0 2.1 collective-permute-done.4
  222.9 10.7 %collective-permute-done.7 = f32[2,32,10,1]{3,2,1,0:T(8,128)S(1)} collective-permute-done((f32[2,32,10,1]{3,2,1,0:T(8,128)S(1)}, f32[2,32,10,1]{3,2,1,0:T(8,128)S(1)}, u32[]{:S(2)}, u32[]{:S(2)}) %collective-permute-start.7) | collective-permute-done | bytes 2592 | tf_op jit(solution)/shard_map/ppermute | solution.py:19
  236.3 20.2 %add_divide_fusion.32 = (f32[1,8,256]{2,1,0:T(8,128)S(1)}, f32[1,8,256]{2,1,0:T(8,128)S(1)}, f32[1,8,256]{2,1,0:T(8,128)S(1)}, f32[1,8,256]{2,1,0:T(8,128)S(1)},...) fusion(f32[32,8,256]{2,1,0:T(8,128)S(1)} %copy-done.6, ...), kind=kLoop, calls=%fused_computation.341 | loop fusion | flops 882688 | bytes 1523836 | tf_op jit(solution)/shard_map/div | solution.py:91
  256.5 2.1 constant_dynamic-update-slice_fusion.70
  259.6 1.6 collective-permute-start.8
  261.3 2.2 collective-permute-done.9
  263.5 1.8 collective-permute-done.8
  266.1 5.8 %collective-permute-done.11 = f32[32,10,1]{2,1,0:T(8,128)S(1)} collective-permute-done((f32[32,10,1]{2,1,0:T(8,128)S(1)}, f32[32,10,1]{2,1,0:T(8,128)S(1)}, u32[]{:S(2)}, u32[]{:S(2)}) %collective-permute-start.11) | collective-permute-done | bytes 1312 | tf_op jit(solution)/shard_map/ppermute | solution.py:19
  271.9 2.0 collective-permute-done.10
  274.9 12.3 %all_to_all.46 = f32[2,32,8,256]{3,2,0,1:T(8,128)S(1)} all-to-all(f32[2,32,8,256]{3,2,0,1:T(8,128)S(1)} %copy.21), channel_id=1, replica_groups=mesh['lat'=4,'lon'=8] {'lon'}, dimensions={1} | all-to-all | bytes 1048576 | tf_op jit(solution)/shard_map/all_to_all | solution.py:57
  288.4 77.2 %fusion.18 = f32[2,4,8,2048]{3,2,1,0:T(8,128)S(1)} fusion(f32[2,4,8,2048]{3,2,1,0:T(8,128)} %all_to_all.40, s32[2048]{0:T(1024)} %copy-done.61, pred[2048]{0:T(1024)(128)(4,1)} %copy-done.63, f32[8,2048]{1,0:T(8,128)} %copy-done.33), kind=kOutput, calls=%fused_computation.22 | convolution fusion | flops 3288465408 | bytes 1124352 | tf_op jit(solution)/shard_map/vetj,jc->vetc/dot_general | solution.py:58
  366.1 82.2 %fusion.3 = f32[2,4,8,2048]{3,2,1,0:T(8,128)S(1)} fusion(f32[2,4,8,2048]{3,2,1,0:T(8,128)S(1)} %fusion.18, s32[2048]{0:T(1024)S(1)} %copy-done.62, pred[2048]{0:T(1024)(128)(4,1)S(1)} %copy-done.64), kind=kOutput, calls=%fused_computation.6 | convolution fusion | flops 3317694464 | bytes 1058816 | tf_op jit(solution)/shard_map/vetc,cj->vetj/dot_general | solution.py:60
  448.4 12.1 %all_to_all.47 = f32[8,2,4,8,256]{4,3,2,1,0:T(8,128)S(1)} all-to-all(f32[8,2,4,8,256]{4,3,2,1,0:T(8,128)S(1)} %constant_dynamic-update-slice_fusion.71), channel_id=1, replica_groups=mesh['lat'=4,'lon'=8] {'lon'}, dimensions={0} | all-to-all | bytes 1048576 | tf_op jit(solution)/shard_map/all_to_all | solution.py:62
  462.0 1.6 collective-permute-start.12
  463.5 2.9 collective-permute-done.13
  466.5 1.6 collective-permute-done.12
  470.0 10.5 %collective-permute-done.15 = f32[2,32,10,1]{3,2,1,0:T(8,128)S(1)} collective-permute-done((f32[2,32,10,1]{3,2,1,0:T(8,128)S(1)}, f32[2,32,10,1]{3,2,1,0:T(8,128)S(1)}, u32[]{:S(2)}, u32[]{:S(2)}) %collective-permute-start.15) | collective-permute-done | bytes 2592 | tf_op jit(solution)/shard_map/ppermute | solution.py:19
  481.8 1.8 maximum_select_fusion.1
  484.9 20.2 %add_divide_fusion.1 = (f32[1,8,256]{2,1,0:T(8,128)S(1)}, f32[1,8,256]{2,1,0:T(8,128)S(1)}, f32[1,8,256]{2,1,0:T(8,128)S(1)}, f32[1,8,256]{2,1,0:T(8,128)S(1)}, ...) fusion(f32[1,8,256]{2,1,0:T(8,128)S(1)} %get-tuple-element.102,, ...), kind=kLoop, calls=%fused_computation.276 | loop fusion | flops 452608 | bytes 1269884 | tf_op jit(solution)/shard_map/div | solution.py:91
  (284 shorter events, 26.4 us)
Async XLA Ops:
  1.8 7.3 %collective-permute-start.1 = (f32[32,1,256]{2,1,0:T(1,128)S(1)}, f32[32,1,256]{2,1,0:T(1,128)S(1)}, u32[]{:S(2)}, u32[]{:S(2)}) collective-permute-start(f32[32,1,256]{2,1,0:T(1,128)S(1)} %get-tuple-element.213), channel_id=1, source_target_pairs={{8,0},{16,8},{24,16},{0,24},{9,1},{17,9},{25,17},{1,25},{10,2},{18... | collective-permute-start | bytes 98312 | tf_op jit(solution)/shard_map/ppermute | solution.py:19
  6.9 5.7 %collective-permute-start = (f32[32,1,256]{2,1,0:T(1,128)S(1)}, f32[32,1,256]{2,1,0:T(1,128)S(1)}, u32[]{:S(2)}, u32[]{:S(2)}) collective-permute-start(f32[32,1,256]{2,1,0:T(1,128)S(1)} %get-tuple-element.212), channel_id=1, source_target_pairs={{0,8},{8,16},{16,24},{24,0},{1,9},{9,17},{17,25},{25,1},{2,10},{10... | collective-permute-start | bytes 98312 | tf_op jit(solution)/shard_map/ppermute | solution.py:16
  12.9 6.7 %collective-permute-start.3 = (f32[32,10,1]{2,1,0:T(8,128)S(1)}, f32[32,10,1]{2,1,0:T(8,128)S(1)}, u32[]{:S(2)}, u32[]{:S(2)}) collective-permute-start(f32[32,10,1]{2,1,0:T(8,128)S(1)} %get-tuple-element.209), channel_id=1, source_target_pairs={{1,0},{2,1},{3,2},{4,3},{5,4},{6,5},{7,6},{0,7},{9,8},{10,9},{11,1... | collective-permute-start | bytes 3848 | tf_op jit(solution)/shard_map/ppermute | solution.py:19
  13.4 9.2 %collective-permute-start.2 = (f32[32,10,1]{2,1,0:T(8,128)S(1)}, f32[32,10,1]{2,1,0:T(8,128)S(1)}, u32[]{:S(2)}, u32[]{:S(2)}) collective-permute-start(f32[32,10,1]{2,1,0:T(8,128)S(1)} %get-tuple-element.208), channel_id=1, source_target_pairs={{0,1},{1,2},{2,3},{3,4},{4,5},{5,6},{6,7},{7,0},{8,9},{9,10},{10,1... | collective-permute-start | bytes 3848 | tf_op jit(solution)/shard_map/ppermute | solution.py:16
  13.4 260.5 %copy-start.65 = (pred[10]{0:T(512)(128)(4,1)}, pred[10]{0:T(512)(128)(4,1)S(1)}, u32[]{:S(2)}) copy-start(pred[10]{0:T(512)(128)(4,1)S(1)} %and_or_fusion) | copy-start | bytes 34
  24.3 13.3 %all-to-all-start = ((f32[2,32,8,256]{3,2,0,1:T(8,128)}), f32[2,32,8,256]{3,2,0,1:T(8,128)S(1)}, u32[]{:S(2)}, u32[]{:S(2)}) async-start(f32[2,32,8,256]{3,2,0,1:T(8,128)} %copy.18), calls=%async_computation | async-start | bytes 1048576 | tf_op jit(solution)/shard_map/all_to_all | solution.py:57
  113.9 122.1 %copy-start = (f32[32,8,256]{2,1,0:T(8,128)S(1)}, f32[32,8,256]{2,1,0:T(8,128)}, u32[]{:S(2)}) copy-start(f32[32,8,256]{2,1,0:T(8,128)} %param.17) | copy-start | bytes 786436
  113.9 122.4 %copy-start.6 = (f32[32,8,256]{2,1,0:T(8,128)S(1)}, f32[32,8,256]{2,1,0:T(8,128)}, u32[]{:S(2)}) copy-start(f32[32,8,256]{2,1,0:T(8,128)} %param.12) | copy-start | bytes 786436
  201.2 13.1 %all-to-all-start.1 = ((f32[8,2,4,8,256]{4,3,2,1,0:T(8,128)}), f32[8,2,4,8,256]{4,3,2,1,0:T(8,128)S(1)}, u32[]{:S(2)}, u32[]{:S(2)}) async-start(f32[8,2,4,8,256]{4,3,2,1,0:T(8,128)} %constant_dynamic-update-slice_fusion), calls=%async_computation.1 | async-start | bytes 1048576 | tf_op jit(solution)/shard_map/all_to_all | solution.py:62
  214.7 4.3 collective-permute-start.5
  215.1 6.1 %collective-permute-start.4 = (f32[2,32,1,256]{3,2,1,0:T(1,128)S(1)}, f32[2,32,1,256]{3,2,1,0:T(1,128)S(1)}, u32[]{:S(2)}, u32[]{:S(2)}) collective-permute-start(f32[2,32,1,256]{3,2,1,0:T(1,128)S(1)} %get-tuple-element.206), channel_id=1, source_target_pairs={{0,8},{8,16},{16,24},{24,0},{1,9},{9,17},{17,25},{25,1},{2,10},{10... | collective-permute-start | bytes 196616 | tf_op jit(solution)/shard_map/ppermute | solution.py:16
  221.5 12.2 %collective-permute-start.7 = (f32[2,32,10,1]{3,2,1,0:T(8,128)S(1)}, f32[2,32,10,1]{3,2,1,0:T(8,128)S(1)}, u32[]{:S(2)}, u32[]{:S(2)}) collective-permute-start(f32[2,32,10,1]{3,2,1,0:T(8,128)S(1)} %get-tuple-element.195), channel_id=1, source_target_pairs={{1,0},{2,1},{3,2},{4,3},{5,4},{6,5},{7,6},{0,7},{9,8},{10,9},{11,1... | collective-permute-start | bytes 7688 | tf_op jit(solution)/shard_map/ppermute | solution.py:19
  221.6 13.3 %collective-permute-start.6 = (f32[2,32,10,1]{3,2,1,0:T(8,128)S(1)}, f32[2,32,10,1]{3,2,1,0:T(8,128)S(1)}, u32[]{:S(2)}, u32[]{:S(2)}) collective-permute-start(f32[2,32,10,1]{3,2,1,0:T(8,128)S(1)} %get-tuple-element.194), channel_id=1, source_target_pairs={{0,1},{1,2},{2,3},{3,4},{4,5},{5,6},{6,7},{7,0},{8,9},{9,10},{10,1... | collective-permute-start | bytes 7688 | tf_op jit(solution)/shard_map/ppermute | solution.py:16
  259.2 4.3 collective-permute-start.9
  259.6 5.7 %collective-permute-start.8 = (f32[32,1,256]{2,1,0:T(1,128)S(1)}, f32[32,1,256]{2,1,0:T(1,128)S(1)}, u32[]{:S(2)}, u32[]{:S(2)}) collective-permute-start(f32[32,1,256]{2,1,0:T(1,128)S(1)} %get-tuple-element.210), channel_id=1, source_target_pairs={{0,8},{8,16},{16,24},{24,0},{1,9},{9,17},{17,25},{25,1},{2,10},{10... | collective-permute-start | bytes 98312 | tf_op jit(solution)/shard_map/ppermute | solution.py:16
  265.6 6.3 %collective-permute-start.11 = (f32[32,10,1]{2,1,0:T(8,128)S(1)}, f32[32,10,1]{2,1,0:T(8,128)S(1)}, u32[]{:S(2)}, u32[]{:S(2)}) collective-permute-start(f32[32,10,1]{2,1,0:T(8,128)S(1)} %get-tuple-element.205), channel_id=1, source_target_pairs={{1,0},{2,1},{3,2},{4,3},{5,4},{6,5},{7,6},{0,7},{9,8},{10,9},{11,1... | collective-permute-start | bytes 3848 | tf_op jit(solution)/shard_map/ppermute | solution.py:19
  265.7 8.2 %collective-permute-start.10 = (f32[32,10,1]{2,1,0:T(8,128)S(1)}, f32[32,10,1]{2,1,0:T(8,128)S(1)}, u32[]{:S(2)}, u32[]{:S(2)}) collective-permute-start(f32[32,10,1]{2,1,0:T(8,128)S(1)} %get-tuple-element.204), channel_id=1, source_target_pairs={{0,1},{1,2},{2,3},{3,4},{4,5},{5,6},{6,7},{7,0},{8,9},{9,10},{10,1... | collective-permute-start | bytes 3848 | tf_op jit(solution)/shard_map/ppermute | solution.py:16
  365.7 118.9 %copy-start.8 = (f32[1,8,256]{2,1,0:T(8,128)S(1)}, f32[1,8,256]{2,1,0:T(8,128)}, u32[]{:S(2)}) copy-start(f32[1,8,256]{2,1,0:T(8,128)} %copy-done.7) | copy-start | bytes 24580
  365.7 118.9 %copy-start.10 = (f32[1,8,256]{2,1,0:T(8,128)S(1)}, f32[1,8,256]{2,1,0:T(8,128)}, u32[]{:S(2)}) copy-start(f32[1,8,256]{2,1,0:T(8,128)} %copy-done.9) | copy-start | bytes 24580
  365.7 118.9 %copy-start.12 = (f32[1,8,256]{2,1,0:T(8,128)S(1)}, f32[1,8,256]{2,1,0:T(8,128)}, u32[]{:S(2)}) copy-start(f32[1,8,256]{2,1,0:T(8,128)} %copy-done.11) | copy-start | bytes 24580
  365.7 118.9 %copy-start.14 = (f32[1,8,256]{2,1,0:T(8,128)S(1)}, f32[1,8,256]{2,1,0:T(8,128)}, u32[]{:S(2)}) copy-start(f32[1,8,256]{2,1,0:T(8,128)} %copy-done.13) | copy-start | bytes 24580
  365.7 118.9 %copy-start.16 = (f32[1,8,256]{2,1,0:T(8,128)S(1)}, f32[1,8,256]{2,1,0:T(8,128)}, u32[]{:S(2)}) copy-start(f32[1,8,256]{2,1,0:T(8,128)} %copy-done.15) | copy-start | bytes 24580
  365.7 118.9 %copy-start.18 = (f32[1,8,256]{2,1,0:T(8,128)S(1)}, f32[1,8,256]{2,1,0:T(8,128)}, u32[]{:S(2)}) copy-start(f32[1,8,256]{2,1,0:T(8,128)} %copy-done.17) | copy-start | bytes 24580
  365.7 118.9 %copy-start.20 = (f32[1,8,256]{2,1,0:T(8,128)S(1)}, f32[1,8,256]{2,1,0:T(8,128)}, u32[]{:S(2)}) copy-start(f32[1,8,256]{2,1,0:T(8,128)} %copy-done.19) | copy-start | bytes 24580
  365.7 118.9 %copy-start.22 = (f32[1,8,256]{2,1,0:T(8,128)S(1)}, f32[1,8,256]{2,1,0:T(8,128)}, u32[]{:S(2)}) copy-start(f32[1,8,256]{2,1,0:T(8,128)} %copy-done.21) | copy-start | bytes 24580
  365.8 118.9 %copy-start.24 = (f32[1,8,256]{2,1,0:T(8,128)S(1)}, f32[1,8,256]{2,1,0:T(8,128)}, u32[]{:S(2)}) copy-start(f32[1,8,256]{2,1,0:T(8,128)} %copy-done.23) | copy-start | bytes 24580
  365.8 118.9 %copy-start.26 = (f32[1,8,256]{2,1,0:T(8,128)S(1)}, f32[1,8,256]{2,1,0:T(8,128)}, u32[]{:S(2)}) copy-start(f32[1,8,256]{2,1,0:T(8,128)} %copy-done.25) | copy-start | bytes 24580
  365.8 118.9 %copy-start.28 = (f32[1,8,256]{2,1,0:T(8,128)S(1)}, f32[1,8,256]{2,1,0:T(8,128)}, u32[]{:S(2)}) copy-start(f32[1,8,256]{2,1,0:T(8,128)} %copy-done.27) | copy-start | bytes 24580
  461.4 5.0 collective-permute-start.13
  462.0 6.1 %collective-permute-start.12 = (f32[2,32,1,256]{3,2,1,0:T(1,128)S(1)}, f32[2,32,1,256]{3,2,1,0:T(1,128)S(1)}, u32[]{:S(2)}, u32[]{:S(2)}) collective-permute-start(f32[2,32,1,256]{3,2,1,0:T(1,128)S(1)} %get-tuple-element.200), channel_id=1, source_target_pairs={{0,8},{8,16},{16,24},{24,0},{1,9},{9,17},{17,25},{25,1},{2,10},{10... | collective-permute-start | bytes 196616 | tf_op jit(solution)/shard_map/ppermute | solution.py:16
  468.4 12.1 %collective-permute-start.15 = (f32[2,32,10,1]{3,2,1,0:T(8,128)S(1)}, f32[2,32,10,1]{3,2,1,0:T(8,128)S(1)}, u32[]{:S(2)}, u32[]{:S(2)}) collective-permute-start(f32[2,32,10,1]{3,2,1,0:T(8,128)S(1)} %get-tuple-element.193), channel_id=1, source_target_pairs={{1,0},{2,1},{3,2},{4,3},{5,4},{6,5},{7,6},{0,7},{9,8},{10,9},{11,1... | collective-permute-start | bytes 7688 | tf_op jit(solution)/shard_map/ppermute | solution.py:19
  468.5 13.3 %collective-permute-start.14 = (f32[2,32,10,1]{3,2,1,0:T(8,128)S(1)}, f32[2,32,10,1]{3,2,1,0:T(8,128)S(1)}, u32[]{:S(2)}, u32[]{:S(2)}) collective-permute-start(f32[2,32,10,1]{3,2,1,0:T(8,128)S(1)} %get-tuple-element.192), channel_id=1, source_target_pairs={{0,1},{1,2},{2,3},{3,4},{4,5},{5,6},{6,7},{7,0},{8,9},{9,10},{10,1... | collective-permute-start | bytes 7688 | tf_op jit(solution)/shard_map/ppermute | solution.py:16
  (57 other events, 4585.3 us)
